TPU v7x, 32 devices: a whole 2x2x4 slice. The times are simulated.
32 devices in a mesh: row: 8 (over z, y), col: 4 (over x, core).
Axes of the slice: x: 2, y: 2, z: 4, core: 2. Of those that a mesh axis runs over, the one named last changes fastest.
Arguments:
- matrix_tiles: bfloat16 [8, 4, 96, 256, 256], P('row', 'col'), may hold values from -0.078125 to 0.078125
- tile_rows: int32 [8, 4, 96], P('row', 'col'), may hold values from 0 to 7, as said below
- tile_cols: int32 [8, 4, 96], P('row', 'col'), may hold values from 0 to 15
- tile_count: int32 [8, 4], P('row', 'col'), may hold values from 24 to 96, as said below
- x_start: float32 [16384, 256], P(('col', 'row')), may hold values from -5 to 5
- y_start: float32 [16384, 256], P(('row', 'col')), may hold values from 0 to 1
- cost_vector: float32 [16384, 256], P(('col', 'row')), may hold values from -6 to 6
- right_side: float32 [16384, 256], P(('row', 'col')), may hold values from -6 to 6
- lower_bound: float32 [16384, 256], P(('col', 'row')), may hold values from -1.5 to -0.3
- upper_bound: float32 [16384, 256], P(('col', 'row')), may hold values from 0.3 to 1.5
- step_primal: float32 [256], replicated, may hold values from 0.2 to 0.45
- step_dual: float32 [256], replicated, may hold values from 0.2 to 0.45
Outputs:
- primal_out: float32 [16384, 256], P(('col', 'row'))
- dual_out: float32 [16384, 256], P(('row', 'col'))
Inputs may be any that keep to these rules, and one draw needn't show every extreme that they name: Within one grid cell the pairs (tile_rows, tile_cols) of its slots are all different. `tile_count`: some grid cell has 96 used slots in every draw; slots at or above a cell's count are not part of A.
All inputs are finite; a program needn't handle non-finite values.
Results may differ from a plain program's by a relative error of at most 0.001.
Values may be sent and summed in bfloat16 or wider, within the bound.
A program may use at most 128 MiB of HBM per device.

v0:
```python
import jax
import jax.numpy as jnp
from jax import lax
from jax.sharding import PartitionSpec as P

NR_DEV = 8
SLOT_BLOCK = 16
eps = 1e-06


def forward_part(my_tiles, my_rows, my_cols, slot_count, segment):
    edge = my_tiles.shape[-1]
    batch_width = segment.shape[-1]
    x_tiles = segment.reshape(-1, edge, batch_width)
    slot_ids = jnp.arange(SLOT_BLOCK, dtype=jnp.int32)

    def forward_block_step(block_index, running):
        first_slot = block_index * SLOT_BLOCK
        tile_block = lax.dynamic_slice_in_dim(my_tiles, first_slot, SLOT_BLOCK, 0)
        row_block = lax.dynamic_slice_in_dim(my_rows, first_slot, SLOT_BLOCK, 0)
        col_block = lax.dynamic_slice_in_dim(my_cols, first_slot, SLOT_BLOCK, 0)
        in_use = first_slot + slot_ids < slot_count
        pieces = jnp.take(x_tiles, col_block, axis=0)
        products = jnp.einsum(
            "sij,sjb->sib", tile_block, pieces, preferred_element_type=jnp.float32
        )
        products = jnp.where(in_use[:, None, None], products, jnp.zeros_like(products))
        return running.at[row_block].add(products)

    blocks = (slot_count + SLOT_BLOCK - 1) // SLOT_BLOCK
    begin = jnp.zeros((NR_DEV, edge, batch_width), jnp.float32)
    return lax.fori_loop(0, blocks, forward_block_step, begin).reshape(-1, batch_width)


def backward_part(my_tiles, my_rows, my_cols, slot_count, segment, col_tiles):
    edge = my_tiles.shape[-1]
    batch_width = segment.shape[-1]
    y_tiles = segment.reshape(-1, edge, batch_width)
    slot_ids = jnp.arange(SLOT_BLOCK, dtype=jnp.int32)

    def backward_block_step(block_index, running):
        first_slot = block_index * SLOT_BLOCK
        tile_block = lax.dynamic_slice_in_dim(my_tiles, first_slot, SLOT_BLOCK, 0)
        row_block = lax.dynamic_slice_in_dim(my_rows, first_slot, SLOT_BLOCK, 0)
        col_block = lax.dynamic_slice_in_dim(my_cols, first_slot, SLOT_BLOCK, 0)
        in_use = first_slot + slot_ids < slot_count
        pieces = jnp.take(y_tiles, row_block, axis=0)
        products = jnp.einsum(
            "sij,sib->sjb", tile_block, pieces, preferred_element_type=jnp.float32
        )
        products = jnp.where(in_use[:, None, None], products, jnp.zeros_like(products))
        return running.at[col_block].add(products)

    blocks = (slot_count + SLOT_BLOCK - 1) // SLOT_BLOCK
    begin = jnp.zeros((col_tiles, edge, batch_width), jnp.float32)
    return lax.fori_loop(0, blocks, backward_block_step, begin).reshape(-1, batch_width)


def body(
    matrix_tiles,
    tile_rows,
    tile_cols,
    tile_count,
    x_start,
    y_start,
    cost_vector,
    right_side,
    lower_bound,
    upper_bound,
    step_primal,
    step_dual,
):
    my_tiles = matrix_tiles[0, 0]
    my_rows = tile_rows[0, 0]
    my_cols = tile_cols[0, 0]
    slot_count = tile_count[0, 0]
    row_devices = lax.axis_size("row")
    col_devices = lax.axis_size("col")
    share = x_start.shape[0]
    edge = my_tiles.shape[-1]
    col_tiles = share * row_devices // edge
    total_cols = share * row_devices * col_devices
    total_rows = y_start.shape[0] * row_devices * col_devices

    def dual_rows(values):
        return lax.all_gather(values.astype(jnp.bfloat16), "col", axis=0, tiled=True)

    def row_sums(segment):
        return lax.psum_scatter(
            forward_part(my_tiles, my_rows, my_cols, slot_count, segment),
            "col",
            scatter_dimension=0,
            tiled=True,
        )

    x_base, cost_seg, lower_seg, upper_seg = (x_start, cost_vector, lower_bound, upper_bound)

    def column_sums(segment):
        partial_value = backward_part(my_tiles, my_rows, my_cols, slot_count, segment, col_tiles)
        return lax.psum_scatter(partial_value, "row", scatter_dimension=0, tiled=True)

    def spread(ahead):
        return lax.all_gather(ahead, "row", axis=0, tiled=True)

    grad_zero = column_sums(dual_rows(y_start))
    primal_one = jnp.clip(x_base - step_primal * (cost_seg - grad_zero), lower_seg, upper_seg)
    primal_diff = primal_one - x_base
    move_primal = jnp.sum(primal_diff * primal_diff, axis=0)
    image_one = row_sums(spread((2.0 * primal_one - x_base).astype(jnp.bfloat16)))
    dual_one = jnp.maximum(y_start + step_dual * (right_side - image_one), 0.0)
    dual_diff = dual_one - y_start
    move_dual = jnp.sum(dual_diff * dual_diff, axis=0)
    move_primal, move_dual = lax.psum((move_primal, move_dual), ("row", "col"))
    weight = jnp.sqrt((move_dual / total_rows + eps) / (move_primal / total_cols + eps))
    grad_one = column_sums(dual_rows(dual_one))
    primal_two = jnp.clip(
        primal_one - step_primal / weight * (cost_seg - grad_one), lower_seg, upper_seg
    )
    image_two = row_sums(spread((2.0 * primal_two - primal_one).astype(jnp.bfloat16)))
    dual_out = jnp.maximum(dual_one + step_dual * weight * (right_side - image_two), 0.0)
    return (primal_two, dual_out)


def solution(mesh):
    placed = (
        P("row", "col", None, None, None),
        P("row", "col", None),
        P("row", "col", None),
        P("row", "col"),
        P(("col", "row"), None),
        P(("row", "col"), None),
        P(("col", "row"), None),
        P(("row", "col"), None),
        P(("col", "row"), None),
        P(("col", "row"), None),
        P(),
        P(),
    )
    return jax.shard_map(
        body,
        mesh=mesh,
        in_specs=placed,
        out_specs=(P(("col", "row"), None), P(("row", "col"), None)),
        check_vma=False,
    )
```

profile of v0, /device:TPU:0, one launch (start us, length us, event | category | flops | bytes accessed | tf_op | source)
XLA Modules:
  0.0 772.5 jit_solution(1718431034138353426)
XLA Ops:
  9.7 16.6 %copy.14 = bf16[96,256,256]{1,2,0:T(8,128)(2,1)} copy(bf16[96,256,256]{2,1,0:T(8,128)(2,1)} %bitcast.19) | data formatting | bytes 25165824
  31.9 91.8 %while.44 = (s32[]{:T(128)}, f32[16,256,256]{2,1,0:T(8,128)}, s32[]{:T(128)}, s32[96]{0:T(128)S(1)}, s32[]{:T(128)}, /*index=5*/bf16[96,256,256]{1,2,0:T(8,128)(...) while((s32[]{:T(128)}, f32[16,256,256]{2,1,0:T(8,128)}, ...), condition=%wide.region_2.4_spmd.clone, body=%wide.region_0.3_spmd.clone.sunk | while | flops 540017856 | bytes 25170616 | solution.py:56
  37.8 9.5 %scatter_fusion = f32[16,256,256]{2,1,0:T(8,128)} fusion(f32[16,256,256]{2,1,0:T(8,128)} %get-tuple-element.615, s32[16]{0:T(128)S(1)} %compare_select_fusion.16, f32[16,256,256]{2,1,0:T(8,128)} %convolution_select_fusion.8), kind=kCustom, calls=%fused_computation.4.clone.clone.1 | custom fusion | flops 1048576 | bytes 12582976 | tf_op jit(solution)/shard_map/while/body/scatter-add | solution.py:52
  53.2 9.5 %scatter_fusion = f32[16,256,256]{2,1,0:T(8,128)} fusion(f32[16,256,256]{2,1,0:T(8,128)} %get-tuple-element.615, s32[16]{0:T(128)S(1)} %compare_select_fusion.16, f32[16,256,256]{2,1,0:T(8,128)} %convolution_select_fusion.8), kind=kCustom, calls=%fused_computation.4.clone.clone.1 | custom fusion | flops 1048576 | bytes 12582976 | tf_op jit(solution)/shard_map/while/body/scatter-add | solution.py:52
  68.5 9.5 %scatter_fusion = f32[16,256,256]{2,1,0:T(8,128)} fusion(f32[16,256,256]{2,1,0:T(8,128)} %get-tuple-element.615, s32[16]{0:T(128)S(1)} %compare_select_fusion.16, f32[16,256,256]{2,1,0:T(8,128)} %convolution_select_fusion.8), kind=kCustom, calls=%fused_computation.4.clone.clone.1 | custom fusion | flops 1048576 | bytes 12582976 | tf_op jit(solution)/shard_map/while/body/scatter-add | solution.py:52
  83.8 9.5 %scatter_fusion = f32[16,256,256]{2,1,0:T(8,128)} fusion(f32[16,256,256]{2,1,0:T(8,128)} %get-tuple-element.615, s32[16]{0:T(128)S(1)} %compare_select_fusion.16, f32[16,256,256]{2,1,0:T(8,128)} %convolution_select_fusion.8), kind=kCustom, calls=%fused_computation.4.clone.clone.1 | custom fusion | flops 1048576 | bytes 12582976 | tf_op jit(solution)/shard_map/while/body/scatter-add | solution.py:52
  114.3 9.5 %scatter_fusion = f32[16,256,256]{2,1,0:T(8,128)} fusion(f32[16,256,256]{2,1,0:T(8,128)} %get-tuple-element.615, s32[16]{0:T(128)S(1)} %compare_select_fusion.16, f32[16,256,256]{2,1,0:T(8,128)} %convolution_select_fusion.8), kind=kCustom, calls=%fused_computation.4.clone.clone.1 | custom fusion | flops 1048576 | bytes 12582976 | tf_op jit(solution)/shard_map/while/body/scatter-add | solution.py:52
  123.8 86.9 %reduce-scatter.5.cloned.1.call-done = f32[512,256]{1,0:T(8,128)} async-done(((f32[4096,256]{1,0:T(8,128)}), f32[512,256]{1,0:T(8,128)}) %reduce-scatter.5.cloned.1.call-update) | async-done | bytes 524304 | tf_op jit(solution)/shard_map/reduce_scatter | solution.py:100
  213.6 48.8 %all-gather.7.cloned.1.call-done = bf16[4096,256]{1,0:T(8,128)(2,1)} async-done(((bf16[512,256]{1,0:T(8,128)(2,1)}), bf16[4096,256]{1,0:T(8,128)(2,1)}) %all-gather.7.cloned.1.call-update) | async-done | bytes 2097168 | tf_op jit(solution)/shard_map/all_gather | solution.py:103
  262.6 93.1 %while.45 = (s32[]{:T(128)}, f32[8,256,256]{2,1,0:T(8,128)S(1)}, s32[]{:T(128)}, s32[96]{0:T(128)S(1)}, s32[]{:T(128)}, /*index=5*/bf16[96,256,256]{2,1,0:T(8,12...) while((s32[]{:T(128)}, f32[8,256,256]{2,1,0:T(8,128)S(1)}, ...), condition=%wide.region_6.9_spmd.clone, body=%wide.region_4.8_spmd.clone.sunk | while | flops 540017856 | bytes 25170616 | solution.py:32
  357.1 28.9 %reduce-scatter.7.cloned.1.call-done = f32[512,256]{1,0:T(8,128)} async-done(((f32[2048,256]{1,0:T(8,128)}), f32[512,256]{1,0:T(8,128)}) %reduce-scatter.7.cloned.1.call-update) | async-done | bytes 524304 | tf_op jit(solution)/shard_map/reduce_scatter | solution.py:89
  388.8 16.8 %all-gather.9.cloned.1.call-done = bf16[2048,256]{1,0:T(8,128)(2,1)} async-done(((bf16[512,256]{1,0:T(8,128)(2,1)}), bf16[2048,256]{1,0:T(8,128)(2,1)}) %all-gather.9.cloned.1.call-update) | async-done | bytes 1048592 | tf_op jit(solution)/shard_map/all_gather | solution.py:86
  408.0 91.8 %while.46 = (s32[]{:T(128)}, f32[16,256,256]{2,1,0:T(8,128)}, s32[]{:T(128)}, s32[96]{0:T(128)S(1)}, s32[]{:T(128)}, /*index=5*/bf16[96,256,256]{1,2,0:T(8,128)(...) while((s32[]{:T(128)}, f32[16,256,256]{2,1,0:T(8,128)}, ...), condition=%wide.region_14.17_spmd.clone, body=%wide.region_12.16_spmd.clone.sunk | while | flops 540017856 | bytes 25170616 | solution.py:56
  413.8 9.5 %scatter_fusion.2 = f32[16,256,256]{2,1,0:T(8,128)} fusion(f32[16,256,256]{2,1,0:T(8,128)} %get-tuple-element.687, s32[16]{0:T(128)S(1)} %compare_select_fusion.18, f32[16,256,256]{2,1,0:T(8,128)} %convolution_select_fusion.10), kind=kCustom, calls=%fused_computation.6.clone.clone.1 | custom fusion | flops 1048576 | bytes 12582976 | tf_op jit(solution)/shard_map/while/body/scatter-add | solution.py:52
  429.2 9.5 %scatter_fusion.2 = f32[16,256,256]{2,1,0:T(8,128)} fusion(f32[16,256,256]{2,1,0:T(8,128)} %get-tuple-element.687, s32[16]{0:T(128)S(1)} %compare_select_fusion.18, f32[16,256,256]{2,1,0:T(8,128)} %convolution_select_fusion.10), kind=kCustom, calls=%fused_computation.6.clone.clone.1 | custom fusion | flops 1048576 | bytes 12582976 | tf_op jit(solution)/shard_map/while/body/scatter-add | solution.py:52
  444.5 9.5 %scatter_fusion.2 = f32[16,256,256]{2,1,0:T(8,128)} fusion(f32[16,256,256]{2,1,0:T(8,128)} %get-tuple-element.687, s32[16]{0:T(128)S(1)} %compare_select_fusion.18, f32[16,256,256]{2,1,0:T(8,128)} %convolution_select_fusion.10), kind=kCustom, calls=%fused_computation.6.clone.clone.1 | custom fusion | flops 1048576 | bytes 12582976 | tf_op jit(solution)/shard_map/while/body/scatter-add | solution.py:52
  459.8 9.5 %scatter_fusion.2 = f32[16,256,256]{2,1,0:T(8,128)} fusion(f32[16,256,256]{2,1,0:T(8,128)} %get-tuple-element.687, s32[16]{0:T(128)S(1)} %compare_select_fusion.18, f32[16,256,256]{2,1,0:T(8,128)} %convolution_select_fusion.10), kind=kCustom, calls=%fused_computation.6.clone.clone.1 | custom fusion | flops 1048576 | bytes 12582976 | tf_op jit(solution)/shard_map/while/body/scatter-add | solution.py:52
  475.1 9.4 %scatter_fusion.2 = f32[16,256,256]{2,1,0:T(8,128)} fusion(f32[16,256,256]{2,1,0:T(8,128)} %get-tuple-element.687, s32[16]{0:T(128)S(1)} %compare_select_fusion.18, f32[16,256,256]{2,1,0:T(8,128)} %convolution_select_fusion.10), kind=kCustom, calls=%fused_computation.6.clone.clone.1 | custom fusion | flops 1048576 | bytes 12582976 | tf_op jit(solution)/shard_map/while/body/scatter-add | solution.py:52
  490.3 9.4 %scatter_fusion.2 = f32[16,256,256]{2,1,0:T(8,128)} fusion(f32[16,256,256]{2,1,0:T(8,128)} %get-tuple-element.687, s32[16]{0:T(128)S(1)} %compare_select_fusion.18, f32[16,256,256]{2,1,0:T(8,128)} %convolution_select_fusion.10), kind=kCustom, calls=%fused_computation.6.clone.clone.1 | custom fusion | flops 1048576 | bytes 12582976 | tf_op jit(solution)/shard_map/while/body/scatter-add | solution.py:52
  499.8 40.9 %all-reduce = (f32[256]{0:T(256)S(1)}, f32[256]{0:T(256)S(1)}) all-reduce(f32[256]{0:T(256)S(1)} %get-tuple-element.372, f32[256]{0:T(256)S(1)} %get-tuple-element.370), channel_id=1, replica_groups=mesh['row'=8,'col'=4] {'row','col'}, use_global_device_ids=true, to_apply=%region_11.14 | all-reduce | flops 512 | bytes 4096 | tf_op jit(solution)/shard_map/psum | solution.py:113
  540.8 47.3 %reduce-scatter.9.cloned.1.call-done = f32[512,256]{1,0:T(8,128)} async-done(((f32[4096,256]{1,0:T(8,128)}), f32[512,256]{1,0:T(8,128)}) %reduce-scatter.9.cloned.1.call-update) | async-done | bytes 524304 | tf_op jit(solution)/shard_map/reduce_scatter | solution.py:100
  590.2 49.3 %all-gather.11.cloned.1.call-done = bf16[4096,256]{1,0:T(8,128)(2,1)} async-done(((bf16[512,256]{1,0:T(8,128)(2,1)}), bf16[4096,256]{1,0:T(8,128)(2,1)}) %all-gather.11.cloned.1.call-update) | async-done | bytes 2097168 | tf_op jit(solution)/shard_map/all_gather | solution.py:103
  639.7 93.7 %while.47 = (s32[]{:T(128)}, f32[8,256,256]{2,1,0:T(8,128)S(1)}, s32[]{:T(128)}, s32[96]{0:T(128)S(1)}, s32[]{:T(128)}, /*index=5*/bf16[96,256,256]{2,1,0:T(8,12...) while((s32[]{:T(128)}, f32[8,256,256]{2,1,0:T(8,128)S(1)}, ...), condition=%wide.region_18.21_spmd.clone, body=%wide.region_16.20_spmd.clone.sunk | while | flops 540017856 | bytes 25170616 | solution.py:32
  734.8 28.9 %reduce-scatter.11.cloned.1.call-done = f32[512,256]{1,0:T(8,128)} async-done(((f32[2048,256]{1,0:T(8,128)}), f32[512,256]{1,0:T(8,128)}) %reduce-scatter.11.cloned.1.call-update) | async-done | bytes 524304 | tf_op jit(solution)/shard_map/reduce_scatter | solution.py:89
  (207 shorter events, 288.1 us)
Async XLA Ops:
  7.2 22.4 %all-gather.5.cloned.1.call-start = ((), (), s32[]{:S(2)}) async-start(), calls=%async_computation.4 | async-start | bytes 1310720 | tf_op jit(solution)/shard_map/all_gather | solution.py:86
  9.0 201.7 %reduce-scatter.5.cloned.1.call-start = ((), (), s32[]{:S(2)}) async-start(), calls=%async_computation.5 | async-start | bytes 4718592 | tf_op jit(solution)/shard_map/reduce_scatter | solution.py:100
  29.6 2.4 copy-start.18
  29.6 2.4 copy-start.19
  123.7 87.0 %copy-start.9 = (f32[512,256]{1,0:T(8,128)S(1)}, f32[512,256]{1,0:T(8,128)}, u32[]{:S(2)}) copy-start(f32[512,256]{1,0:T(8,128)} %param.33) | copy-start | bytes 1572868
  123.7 87.0 %copy-start.11 = (f32[512,256]{1,0:T(8,128)S(1)}, f32[512,256]{1,0:T(8,128)}, u32[]{:S(2)}) copy-start(f32[512,256]{1,0:T(8,128)} %param.32) | copy-start | bytes 1572868
  123.7 87.0 %copy-start.13 = (f32[512,256]{1,0:T(8,128)S(1)}, f32[512,256]{1,0:T(8,128)}, u32[]{:S(2)}) copy-start(f32[512,256]{1,0:T(8,128)} %param.30) | copy-start | bytes 1572868
  123.7 87.0 %copy-start.17 = (f32[512,256]{1,0:T(8,128)S(1)}, f32[512,256]{1,0:T(8,128)}, u32[]{:S(2)}) copy-start(f32[512,256]{1,0:T(8,128)} %param.28) | copy-start | bytes 1572868
  123.8 87.0 %copy-start.21 = (f32[256]{0:T(256)S(1)}, f32[256]{0:T(256)}, u32[]{:S(2)}) copy-start(f32[256]{0:T(256)} %param.34) | copy-start | bytes 3076
  123.8 138.6 %all-gather.7.cloned.1.call-start = ((), (), s32[]{:S(2)}) async-start(), calls=%async_computation.6 | async-start | bytes 2359296 | tf_op jit(solution)/shard_map/all_gather | solution.py:103
  213.5 172.5 %reduce-scatter.7.cloned.1.call-start = ((), (), s32[]{:S(2)}) async-start(), calls=%async_computation.7 | async-start | bytes 2621440 | tf_op jit(solution)/shard_map/reduce_scatter | solution.py:89
  355.7 30.3 %copy-start.8 = (f32[512,256]{1,0:T(8,128)S(1)}, f32[512,256]{1,0:T(8,128)}, u32[]{:S(2)}) copy-start(f32[512,256]{1,0:T(8,128)} %param.29) | copy-start | bytes 1572868
  355.7 30.2 %copy-start.15 = (f32[512,256]{1,0:T(8,128)S(1)}, f32[512,256]{1,0:T(8,128)}, u32[]{:S(2)}) copy-start(f32[512,256]{1,0:T(8,128)} %param.31) | copy-start | bytes 1572868
  355.8 30.2 %copy-start.20 = (f32[256]{0:T(256)S(1)}, f32[256]{0:T(256)}, u32[]{:S(2)}) copy-start(f32[256]{0:T(256)} %param.35) | copy-start | bytes 3076
  357.1 48.6 %all-gather.9.cloned.1.call-start = ((), (), s32[]{:S(2)}) async-start(), calls=%async_computation.8 | async-start | bytes 1310720 | tf_op jit(solution)/shard_map/all_gather | solution.py:86
  388.7 199.3 %reduce-scatter.9.cloned.1.call-start = ((), (), s32[]{:S(2)}) async-start(), calls=%async_computation.9 | async-start | bytes 4718592 | tf_op jit(solution)/shard_map/reduce_scatter | solution.py:100
  499.8 88.3 %copy-start.7 = (f32[512,256]{1,0:T(8,128)S(1)}, f32[512,256]{1,0:T(8,128)}, u32[]{:S(2)}) copy-start(f32[512,256]{1,0:T(8,128)} %copy-done.6) | copy-start | bytes 1572868
  499.8 88.3 %copy-start.10 = (f32[512,256]{1,0:T(8,128)S(1)}, f32[512,256]{1,0:T(8,128)}, u32[]{:S(2)}) copy-start(f32[512,256]{1,0:T(8,128)} %param.33) | copy-start | bytes 1572868
  499.8 88.3 %copy-start.12 = (f32[512,256]{1,0:T(8,128)S(1)}, f32[512,256]{1,0:T(8,128)}, u32[]{:S(2)}) copy-start(f32[512,256]{1,0:T(8,128)} %param.32) | copy-start | bytes 1572868
  499.8 88.3 %copy-start.14 = (f32[512,256]{1,0:T(8,128)S(1)}, f32[512,256]{1,0:T(8,128)}, u32[]{:S(2)}) copy-start(f32[512,256]{1,0:T(8,128)} %param.30) | copy-start | bytes 1572868
  499.8 139.7 %all-gather.11.cloned.1.call-start = ((), (), s32[]{:S(2)}) async-start(), calls=%async_computation.10 | async-start | bytes 2359296 | tf_op jit(solution)/shard_map/all_gather | solution.py:103
  590.2 173.5 %reduce-scatter.11.cloned.1.call-start = ((), (), s32[]{:S(2)}) async-start(), calls=%async_computation.11 | async-start | bytes 2621440 | tf_op jit(solution)/shard_map/reduce_scatter | solution.py:89
  733.4 30.3 %copy-start.5 = (f32[512,256]{1,0:T(8,128)S(1)}, f32[512,256]{1,0:T(8,128)}, u32[]{:S(2)}) copy-start(f32[512,256]{1,0:T(8,128)} %copy-done.4) | copy-start | bytes 1572868
  733.4 30.3 %copy-start.16 = (f32[512,256]{1,0:T(8,128)S(1)}, f32[512,256]{1,0:T(8,128)}, u32[]{:S(2)}) copy-start(f32[512,256]{1,0:T(8,128)} %param.31) | copy-start | bytes 1572868
  (6 other events, 9.0 us)
Sparse Core Ops, SparseCore 0:
  10.1 19.4 all-gather.4
  123.9 86.7 reduce-scatter.4
  213.6 48.7 all-gather.6
  357.2 28.7 reduce-scatter.6
  388.9 16.7 all-gather.8
  499.9 88.0 reduce-scatter.8
  590.8 48.7 all-gather.10
  734.9 28.7 reduce-scatter.10
where the time goes:
time: 775 us; the launch traced here: 772 us
  waiting for transfers between devices  310 us (40%)
  other arithmetic  217 us (28%)
  matrix products  111 us (14%)
  local copies, waits for them, and re-layouts  77.6 us (10%)
  blocking collectives  40.9 us (5%)
  between operations  15 us (2%)
    reduce_scatter x2, waiting for transfers between devices, column_sums(): lax.psum_scatter(partial_value, 'row', scatter_dimension=0, tiled=True)  134 us
    scatter-add x12, other arithmetic, backward_block_step(): return running.at[col_block].add(products)  114 us
    all_gather x2, waiting for transfers between devices, spread(): return lax.all_gather(ahead, 'row', axis=0, tiled=True)  98.1 us
    scatter-add x12, other arithmetic, forward_block_step(): return running.at[row_block].add(products)  73.9 us
    dot_general x12, matrix products, forward_block_step(): jnp.einsum('sij,sjb->sib', tile_block, pieces, preferred_element_type=jnp...  59.4 us
    reduce_scatter x2, waiting for transfers between devices, row_sums(): lax.psum_scatter(forward_part(my_tiles, my_rows, my_cols, slot_count, seg...  57.8 us
    dot_general x12, matrix products, backward_block_step(): jnp.einsum('sij,sib->sjb', tile_block, pieces, preferred_element_type=jnp...  51.9 us
    gather x12, local copies, waits for them, and re-layouts, forward_block_step(): pieces = jnp.take(x_tiles, col_block, axis=0)  43.4 us
  transfers between devices with their start and end apart: 8, of which 8 were waited for; matrix products, arithmetic and copies ran while one was open for 2% of the time, Pallas kernels for 0%

commit v1 on v0

--- a/solution.py
+++ b/solution.py
@@ -6,6 +6,29 @@
 NR_DEV = 8
 SLOT_BLOCK = 16
 eps = 1e-06
+
+
+def ratios_move(field, dim_at):
+    aux = list(field.shape[1:])
+    aux[dim_at] *= field.shape[0]
+    return jnp.moveaxis(field, 0, dim_at).reshape(aux)
+
+
+def remake_threads_on_mesh(x_in, ax_name):
+    a_now, block_last = (jax.lax.axis_size(ax_name), jax.lax.axis_index(ax_name))
+    t_next, known = (x_in[None], 1)
+    while known < a_now:
+        extra = jax.lax.ppermute(
+            t_next, axis_name=ax_name, perm=tuple(((i0, i0 ^ known) for i0 in range(a_now)))
+        )
+        val = block_last & known == 0
+        t_next = jnp.concatenate([jnp.where(val, t_next, extra), jnp.where(val, extra, t_next)])
+        known *= 2
+    return t_next
+
+
+def windows_watch(q_in, work_x, k_dim=0):
+    return ratios_move(remake_threads_on_mesh(q_in, work_x), k_dim)
 
 
 def forward_part(my_tiles, my_rows, my_cols, slot_count, segment):
@@ -100,7 +123,7 @@
         return lax.psum_scatter(partial_value, "row", scatter_dimension=0, tiled=True)
 
     def spread(ahead):
-        return lax.all_gather(ahead, "row", axis=0, tiled=True)
+        return windows_watch(ahead, "row")
 
     grad_zero = column_sums(dual_rows(y_start))
     primal_one = jnp.clip(x_base - step_primal * (cost_seg - grad_zero), lower_seg, upper_seg)

time: 775 us -> 817 us (1.054)
  waiting for transfers between devices: 310 us -> 335 us
  starting transfers between devices: 0.33 us -> 12.3 us
    ppermute x0 -> x6, waiting for transfers between devices: none -> 122 us  [remake_threads_on_mesh(): jax.lax.ppermute(t_next, axis_name=ax_name, perm=tuple(((i0, i0 ^ known)...]
    all_gather x2 -> x0, waiting for transfers between devices: 98.1 us -> none  [spread(): return lax.all_gather(ahead, 'row', axis=0, tiled=True)]
    ppermute x0 -> x6, starting transfers between devices: none -> 12.1 us  [remake_threads_on_mesh(): jax.lax.ppermute(t_next, axis_name=ax_name, perm=tuple(((i0, i0 ^ known)...]
  transfers between devices with their start and end apart: 8 -> 12, of which waited for: 8 -> 12; matrix products, arithmetic and copies ran while one was open for 2% -> 2% of each run, Pallas kernels for 0% -> 0%
where the time goes in v1:
time: 817 us; the launch traced here: 814 us
  waiting for transfers between devices  335 us (41%)
  other arithmetic  220 us (27%)
  matrix products  112 us (14%)
  local copies, waits for them, and re-layouts  77.8 us (10%)
  blocking collectives  41.2 us (5%)
  between operations  15 us (2%)
  starting transfers between devices  12.3 us (2%)
    reduce_scatter x2, waiting for transfers between devices, column_sums(): lax.psum_scatter(partial_value, 'row', scatter_dimension=0, tiled=True)  134 us
    ppermute x6, waiting for transfers between devices, remake_threads_on_mesh(): jax.lax.ppermute(t_next, axis_name=ax_name, perm=tuple(((i0, i0 ^ known)...  122 us
    scatter-add x12, other arithmetic, backward_block_step(): return running.at[col_block].add(products)  114 us
    scatter-add x12, other arithmetic, forward_block_step(): return running.at[row_block].add(products)  73.9 us
    reduce_scatter x2, waiting for transfers between devices, row_sums(): lax.psum_scatter(forward_part(my_tiles, my_rows, my_cols, slot_count, seg...  59.7 us
    dot_general x12, matrix products, forward_block_step(): jnp.einsum('sij,sjb->sib', tile_block, pieces, preferred_element_type=jnp...  59.6 us
    dot_general x12, matrix products, backward_block_step(): jnp.einsum('sij,sib->sjb', tile_block, pieces, preferred_element_type=jnp...  52.1 us
    gather x12, local copies, waits for them, and re-layouts, forward_block_step(): pieces = jnp.take(x_tiles, col_block, axis=0)  43.5 us
  transfers between devices with their start and end apart: 12, of which 12 were waited for; matrix products, arithmetic and copies ran while one was open for 2% of the time, Pallas kernels for 0%

profile of v1, /device:TPU:0, one launch (start us, length us, event | category | flops | bytes accessed | tf_op | source)
XLA Modules:
  0.0 813.7 jit_solution(17416020310370027735)
XLA Ops:
  9.7 16.7 %copy.14 = bf16[96,256,256]{1,2,0:T(8,128)(2,1)} copy(bf16[96,256,256]{2,1,0:T(8,128)(2,1)} %bitcast.23) | data formatting | bytes 25165824
  32.0 91.9 %while.44 = (s32[]{:T(128)}, f32[16,256,256]{2,1,0:T(8,128)}, s32[]{:T(128)}, s32[96]{0:T(128)S(1)}, s32[]{:T(128)}, /*index=5*/bf16[96,256,256]{1,2,0:T(8,128)(...) while((s32[]{:T(128)}, f32[16,256,256]{2,1,0:T(8,128)}, ...), condition=%wide.region_2.4_spmd.clone, body=%wide.region_0.3_spmd.clone.sunk | while | flops 540017856 | bytes 25170616 | solution.py:79
  37.8 9.6 %scatter_fusion = f32[16,256,256]{2,1,0:T(8,128)} fusion(f32[16,256,256]{2,1,0:T(8,128)} %get-tuple-element.627, s32[16]{0:T(128)S(1)} %compare_select_fusion.16, f32[16,256,256]{2,1,0:T(8,128)} %convolution_select_fusion.8), kind=kCustom, calls=%fused_computation.4.clone.clone.1 | custom fusion | flops 1048576 | bytes 12582976 | tf_op jit(solution)/shard_map/while/body/scatter-add | solution.py:75
  53.2 9.5 %scatter_fusion = f32[16,256,256]{2,1,0:T(8,128)} fusion(f32[16,256,256]{2,1,0:T(8,128)} %get-tuple-element.627, s32[16]{0:T(128)S(1)} %compare_select_fusion.16, f32[16,256,256]{2,1,0:T(8,128)} %convolution_select_fusion.8), kind=kCustom, calls=%fused_computation.4.clone.clone.1 | custom fusion | flops 1048576 | bytes 12582976 | tf_op jit(solution)/shard_map/while/body/scatter-add | solution.py:75
  68.6 9.5 %scatter_fusion = f32[16,256,256]{2,1,0:T(8,128)} fusion(f32[16,256,256]{2,1,0:T(8,128)} %get-tuple-element.627, s32[16]{0:T(128)S(1)} %compare_select_fusion.16, f32[16,256,256]{2,1,0:T(8,128)} %convolution_select_fusion.8), kind=kCustom, calls=%fused_computation.4.clone.clone.1 | custom fusion | flops 1048576 | bytes 12582976 | tf_op jit(solution)/shard_map/while/body/scatter-add | solution.py:75
  83.9 9.5 %scatter_fusion = f32[16,256,256]{2,1,0:T(8,128)} fusion(f32[16,256,256]{2,1,0:T(8,128)} %get-tuple-element.627, s32[16]{0:T(128)S(1)} %compare_select_fusion.16, f32[16,256,256]{2,1,0:T(8,128)} %convolution_select_fusion.8), kind=kCustom, calls=%fused_computation.4.clone.clone.1 | custom fusion | flops 1048576 | bytes 12582976 | tf_op jit(solution)/shard_map/while/body/scatter-add | solution.py:75
  114.4 9.5 %scatter_fusion = f32[16,256,256]{2,1,0:T(8,128)} fusion(f32[16,256,256]{2,1,0:T(8,128)} %get-tuple-element.627, s32[16]{0:T(128)S(1)} %compare_select_fusion.16, f32[16,256,256]{2,1,0:T(8,128)} %convolution_select_fusion.8), kind=kCustom, calls=%fused_computation.4.clone.clone.1 | custom fusion | flops 1048576 | bytes 12582976 | tf_op jit(solution)/shard_map/while/body/scatter-add | solution.py:75
  124.0 87.0 %reduce-scatter.5.cloned.1.call-done = f32[512,256]{1,0:T(8,128)} async-done(((f32[4096,256]{1,0:T(8,128)}), f32[512,256]{1,0:T(8,128)}) %reduce-scatter.5.cloned.1.call-update) | async-done | bytes 524304 | tf_op jit(solution)/shard_map/reduce_scatter | solution.py:123
  222.7 10.7 %collective-permute-done.1 = bf16[2,512,256]{2,1,0:T(8,128)(2,1)S(1)} collective-permute-done((bf16[2,512,256]{2,1,0:T(8,128)(2,1)S(1)}, bf16[2,512,256]{2,1,0:T(8,128)(2,1)S(1)}, u32[]{:S(2)}, u32[]{:S(2)}) %collective-permute-start.1) | collective-permute-done | bytes 524320 | tf_op jit(solution)/shard_map/ppermute | solution.py:21
  236.4 43.9 %collective-permute-done.2 = bf16[4,512,256]{2,1,0:T(8,128)(2,1)S(1)} collective-permute-done((bf16[4,512,256]{2,1,0:T(8,128)(2,1)S(1)}, bf16[4,512,256]{2,1,0:T(8,128)(2,1)S(1)}, u32[]{:S(2)}, u32[]{:S(2)}) %collective-permute-start.2) | collective-permute-done | bytes 1048608 | tf_op jit(solution)/shard_map/ppermute | solution.py:21
  282.1 93.3 %while.45 = (s32[]{:T(128)}, f32[8,256,256]{2,1,0:T(8,128)S(1)}, s32[]{:T(128)}, s32[96]{0:T(128)S(1)}, s32[]{:T(128)}, /*index=5*/bf16[96,256,256]{2,1,0:T(8,12...) while((s32[]{:T(128)}, f32[8,256,256]{2,1,0:T(8,128)S(1)}, ...), condition=%wide.region_6.9_spmd.clone, body=%wide.region_4.8_spmd.clone.sunk | while | flops 540017856 | bytes 25170616 | solution.py:55
  376.8 29.8 %reduce-scatter.7.cloned.1.call-done = f32[512,256]{1,0:T(8,128)} async-done(((f32[2048,256]{1,0:T(8,128)}), f32[512,256]{1,0:T(8,128)}) %reduce-scatter.7.cloned.1.call-update) | async-done | bytes 524304 | tf_op jit(solution)/shard_map/reduce_scatter | solution.py:112
  409.4 16.8 %all-gather.5.cloned.1.call-done = bf16[2048,256]{1,0:T(8,128)(2,1)} async-done(((bf16[512,256]{1,0:T(8,128)(2,1)}), bf16[2048,256]{1,0:T(8,128)(2,1)}) %all-gather.5.cloned.1.call-update) | async-done | bytes 1048592 | tf_op jit(solution)/shard_map/all_gather | solution.py:109
  428.6 91.9 %while.46 = (s32[]{:T(128)}, f32[16,256,256]{2,1,0:T(8,128)}, s32[]{:T(128)}, s32[96]{0:T(128)S(1)}, s32[]{:T(128)}, /*index=5*/bf16[96,256,256]{1,2,0:T(8,128)(...) while((s32[]{:T(128)}, f32[16,256,256]{2,1,0:T(8,128)}, ...), condition=%wide.region_14.17_spmd.clone, body=%wide.region_12.16_spmd.clone.sunk | while | flops 540017856 | bytes 25170616 | solution.py:79
  434.5 9.5 %scatter_fusion.2 = f32[16,256,256]{2,1,0:T(8,128)} fusion(f32[16,256,256]{2,1,0:T(8,128)} %get-tuple-element.699, s32[16]{0:T(128)S(1)} %compare_select_fusion.18, f32[16,256,256]{2,1,0:T(8,128)} %convolution_select_fusion.10), kind=kCustom, calls=%fused_computation.6.clone.clone.1 | custom fusion | flops 1048576 | bytes 12582976 | tf_op jit(solution)/shard_map/while/body/scatter-add | solution.py:75
  449.8 9.6 %scatter_fusion.2 = f32[16,256,256]{2,1,0:T(8,128)} fusion(f32[16,256,256]{2,1,0:T(8,128)} %get-tuple-element.699, s32[16]{0:T(128)S(1)} %compare_select_fusion.18, f32[16,256,256]{2,1,0:T(8,128)} %convolution_select_fusion.10), kind=kCustom, calls=%fused_computation.6.clone.clone.1 | custom fusion | flops 1048576 | bytes 12582976 | tf_op jit(solution)/shard_map/while/body/scatter-add | solution.py:75
  465.2 9.5 %scatter_fusion.2 = f32[16,256,256]{2,1,0:T(8,128)} fusion(f32[16,256,256]{2,1,0:T(8,128)} %get-tuple-element.699, s32[16]{0:T(128)S(1)} %compare_select_fusion.18, f32[16,256,256]{2,1,0:T(8,128)} %convolution_select_fusion.10), kind=kCustom, calls=%fused_computation.6.clone.clone.1 | custom fusion | flops 1048576 | bytes 12582976 | tf_op jit(solution)/shard_map/while/body/scatter-add | solution.py:75
  511.1 9.5 %scatter_fusion.2 = f32[16,256,256]{2,1,0:T(8,128)} fusion(f32[16,256,256]{2,1,0:T(8,128)} %get-tuple-element.699, s32[16]{0:T(128)S(1)} %compare_select_fusion.18, f32[16,256,256]{2,1,0:T(8,128)} %convolution_select_fusion.10), kind=kCustom, calls=%fused_computation.6.clone.clone.1 | custom fusion | flops 1048576 | bytes 12582976 | tf_op jit(solution)/shard_map/while/body/scatter-add | solution.py:75
  520.7 41.2 %all-reduce = (f32[256]{0:T(256)S(1)}, f32[256]{0:T(256)S(1)}) all-reduce(f32[256]{0:T(256)S(1)} %get-tuple-element.372, f32[256]{0:T(256)S(1)} %get-tuple-element.370), channel_id=1, replica_groups=mesh['row'=8,'col'=4] {'row','col'}, use_global_device_ids=true, to_apply=%region_11.14 | all-reduce | flops 512 | bytes 4096 | tf_op jit(solution)/shard_map/psum | solution.py:136
  561.9 46.9 %reduce-scatter.9.cloned.1.call-done = f32[512,256]{1,0:T(8,128)} async-done(((f32[4096,256]{1,0:T(8,128)}), f32[512,256]{1,0:T(8,128)}) %reduce-scatter.9.cloned.1.call-update) | async-done | bytes 524304 | tf_op jit(solution)/shard_map/reduce_scatter | solution.py:123
  620.3 10.7 %collective-permute-done.4 = bf16[2,512,256]{2,1,0:T(8,128)(2,1)S(1)} collective-permute-done((bf16[2,512,256]{2,1,0:T(8,128)(2,1)S(1)}, bf16[2,512,256]{2,1,0:T(8,128)(2,1)S(1)}, u32[]{:S(2)}, u32[]{:S(2)}) %collective-permute-start.4) | collective-permute-done | bytes 524320 | tf_op jit(solution)/shard_map/ppermute | solution.py:21
  634.0 43.9 %collective-permute-done.5 = bf16[4,512,256]{2,1,0:T(8,128)(2,1)S(1)} collective-permute-done((bf16[4,512,256]{2,1,0:T(8,128)(2,1)S(1)}, bf16[4,512,256]{2,1,0:T(8,128)(2,1)S(1)}, u32[]{:S(2)}, u32[]{:S(2)}) %collective-permute-start.5) | collective-permute-done | bytes 1048608 | tf_op jit(solution)/shard_map/ppermute | solution.py:21
  679.7 93.8 %while.47 = (s32[]{:T(128)}, f32[8,256,256]{2,1,0:T(8,128)S(1)}, s32[]{:T(128)}, s32[96]{0:T(128)S(1)}, s32[]{:T(128)}, /*index=5*/bf16[96,256,256]{2,1,0:T(8,12...) while((s32[]{:T(128)}, f32[8,256,256]{2,1,0:T(8,128)S(1)}, ...), condition=%wide.region_18.21_spmd.clone, body=%wide.region_16.20_spmd.clone.sunk | while | flops 540017856 | bytes 25170616 | solution.py:55
  774.9 29.9 %reduce-scatter.11.cloned.1.call-done = f32[512,256]{1,0:T(8,128)} async-done(((f32[2048,256]{1,0:T(8,128)}), f32[512,256]{1,0:T(8,128)}) %reduce-scatter.11.cloned.1.call-update) | async-done | bytes 524304 | tf_op jit(solution)/shard_map/reduce_scatter | solution.py:112
  (225 shorter events, 335.0 us)
Async XLA Ops:
  7.2 22.4 %all-gather.3.cloned.1.call-start = ((), (), s32[]{:S(2)}) async-start(), calls=%async_computation.4 | async-start | bytes 1310720 | tf_op jit(solution)/shard_map/all_gather | solution.py:109
  9.0 202.0 %reduce-scatter.5.cloned.1.call-start = ((), (), s32[]{:S(2)}) async-start(), calls=%async_computation.5 | async-start | bytes 4718592 | tf_op jit(solution)/shard_map/reduce_scatter | solution.py:123
  123.9 87.1 %copy-start.9 = (f32[512,256]{1,0:T(8,128)S(1)}, f32[512,256]{1,0:T(8,128)}, u32[]{:S(2)}) copy-start(f32[512,256]{1,0:T(8,128)} %param.33) | copy-start | bytes 1572868
  123.9 87.1 %copy-start.11 = (f32[512,256]{1,0:T(8,128)S(1)}, f32[512,256]{1,0:T(8,128)}, u32[]{:S(2)}) copy-start(f32[512,256]{1,0:T(8,128)} %param.32) | copy-start | bytes 1572868
  123.9 87.1 %copy-start.13 = (f32[512,256]{1,0:T(8,128)S(1)}, f32[512,256]{1,0:T(8,128)}, u32[]{:S(2)}) copy-start(f32[512,256]{1,0:T(8,128)} %param.30) | copy-start | bytes 1572868
  123.9 87.1 %copy-start.17 = (f32[512,256]{1,0:T(8,128)S(1)}, f32[512,256]{1,0:T(8,128)}, u32[]{:S(2)}) copy-start(f32[512,256]{1,0:T(8,128)} %param.28) | copy-start | bytes 1572868
  123.9 87.1 %copy-start.21 = (f32[256]{0:T(256)S(1)}, f32[256]{0:T(256)}, u32[]{:S(2)}) copy-start(f32[256]{0:T(256)} %param.34) | copy-start | bytes 3076
  123.9 282.7 %reduce-scatter.7.cloned.1.call-start = ((), (), s32[]{:S(2)}) async-start(), calls=%async_computation.6 | async-start | bytes 2621440 | tf_op jit(solution)/shard_map/reduce_scatter | solution.py:112
  213.1 7.7 collective-permute-start
  220.9 12.5 %collective-permute-start.1 = (bf16[2,512,256]{2,1,0:T(8,128)(2,1)S(1)}, bf16[2,512,256]{2,1,0:T(8,128)(2,1)S(1)}, u32[]{:S(2)}, u32[]{:S(2)}) collective-permute-start(bf16[2,512,256]{2,1,0:T(8,128)(2,1)S(1)} %pad_maximum_fusion.4), channel_id=1, source_target_pairs={{0,8},{4,12},{8,0},{12,4},{16,24},{20,28},{24,16},{28,20},{1,9},{5... | collective-permute-start | bytes 1572872 | tf_op jit(solution)/shard_map/ppermute | solution.py:21
  233.6 46.6 %collective-permute-start.2 = (bf16[4,512,256]{2,1,0:T(8,128)(2,1)S(1)}, bf16[4,512,256]{2,1,0:T(8,128)(2,1)S(1)}, u32[]{:S(2)}, u32[]{:S(2)}) collective-permute-start(bf16[4,512,256]{2,1,0:T(8,128)(2,1)S(1)} %pad_maximum_fusion.2), channel_id=1, source_target_pairs={{0,16},{4,20},{8,24},{12,28},{16,0},{20,4},{24,8},{28,12},{1,17},{... | collective-permute-start | bytes 3145736 | tf_op jit(solution)/shard_map/ppermute | solution.py:21
  375.5 31.2 %copy-start.8 = (f32[512,256]{1,0:T(8,128)S(1)}, f32[512,256]{1,0:T(8,128)}, u32[]{:S(2)}) copy-start(f32[512,256]{1,0:T(8,128)} %param.29) | copy-start | bytes 1572868
  376.8 49.5 %all-gather.5.cloned.1.call-start = ((), (), s32[]{:S(2)}) async-start(), calls=%async_computation.7 | async-start | bytes 1310720 | tf_op jit(solution)/shard_map/all_gather | solution.py:109
  409.4 199.4 %reduce-scatter.9.cloned.1.call-start = ((), (), s32[]{:S(2)}) async-start(), calls=%async_computation.8 | async-start | bytes 4718592 | tf_op jit(solution)/shard_map/reduce_scatter | solution.py:123
  520.6 88.2 %copy-start.5 = (f32[512,256]{1,0:T(8,128)S(1)}, f32[512,256]{1,0:T(8,128)}, u32[]{:S(2)}) copy-start(f32[512,256]{1,0:T(8,128)} %copy-done.4) | copy-start | bytes 1572868
  520.6 88.2 %copy-start.10 = (f32[512,256]{1,0:T(8,128)S(1)}, f32[512,256]{1,0:T(8,128)}, u32[]{:S(2)}) copy-start(f32[512,256]{1,0:T(8,128)} %param.33) | copy-start | bytes 1572868
  520.6 88.2 %copy-start.12 = (f32[512,256]{1,0:T(8,128)S(1)}, f32[512,256]{1,0:T(8,128)}, u32[]{:S(2)}) copy-start(f32[512,256]{1,0:T(8,128)} %param.32) | copy-start | bytes 1572868
  520.6 88.2 %copy-start.14 = (f32[512,256]{1,0:T(8,128)S(1)}, f32[512,256]{1,0:T(8,128)}, u32[]{:S(2)}) copy-start(f32[512,256]{1,0:T(8,128)} %param.30) | copy-start | bytes 1572868
  520.6 284.3 %reduce-scatter.11.cloned.1.call-start = ((), (), s32[]{:S(2)}) async-start(), calls=%async_computation.9 | async-start | bytes 2621440 | tf_op jit(solution)/shard_map/reduce_scatter | solution.py:112
  610.8 7.7 collective-permute-start.3
  618.6 12.5 %collective-permute-start.4 = (bf16[2,512,256]{2,1,0:T(8,128)(2,1)S(1)}, bf16[2,512,256]{2,1,0:T(8,128)(2,1)S(1)}, u32[]{:S(2)}, u32[]{:S(2)}) collective-permute-start(bf16[2,512,256]{2,1,0:T(8,128)(2,1)S(1)} %pad_maximum_fusion.5), channel_id=1, source_target_pairs={{0,8},{4,12},{8,0},{12,4},{16,24},{20,28},{24,16},{28,20},{1,9},{5... | collective-permute-start | bytes 1572872 | tf_op jit(solution)/shard_map/ppermute | solution.py:21
  631.2 46.6 %collective-permute-start.5 = (bf16[4,512,256]{2,1,0:T(8,128)(2,1)S(1)}, bf16[4,512,256]{2,1,0:T(8,128)(2,1)S(1)}, u32[]{:S(2)}, u32[]{:S(2)}) collective-permute-start(bf16[4,512,256]{2,1,0:T(8,128)(2,1)S(1)} %pad_maximum_fusion.3), channel_id=1, source_target_pairs={{0,16},{4,20},{8,24},{12,28},{16,0},{20,4},{24,8},{28,12},{1,17},{... | collective-permute-start | bytes 3145736 | tf_op jit(solution)/shard_map/ppermute | solution.py:21
  773.6 31.3 %copy-start.7 = (f32[512,256]{1,0:T(8,128)S(1)}, f32[512,256]{1,0:T(8,128)}, u32[]{:S(2)}) copy-start(f32[512,256]{1,0:T(8,128)} %copy-done.6) | copy-start | bytes 1572868
  773.6 31.3 %copy-start.16 = (f32[512,256]{1,0:T(8,128)S(1)}, f32[512,256]{1,0:T(8,128)}, u32[]{:S(2)}) copy-start(f32[512,256]{1,0:T(8,128)} %param.31) | copy-start | bytes 1572868
  (10 other events, 76.2 us)
Sparse Core Ops, SparseCore 0:
  10.1 19.4 all-gather.2
  124.1 86.9 reduce-scatter.4
  376.9 29.6 reduce-scatter.6
  409.5 16.6 all-gather.4
  520.7 87.9 reduce-scatter.8
  775.1 29.7 reduce-scatter.10
